TPU v7x, 32 devices: a whole 2x2x4 slice. The times are simulated.
32 devices in a mesh: dp: 2 (over x), vocab: 16 (over z, y, core).
Axes of the slice: x: 2, y: 2, z: 4, core: 2. Of those that a mesh axis runs over, the one named last changes fastest.
Arguments:
- hidden: bfloat16 [1536, 4096], P(('dp', 'vocab')), may hold values from -75 to 75
- embedding: bfloat16 [8192, 4096], P(('dp', 'vocab')), may hold values from -0.5 to 0.5
- targets: int32 [1536], replicated, may hold values from 0 to 8191
Outputs:
- token_loss: float32 [1536], P(('dp', 'vocab'))
- mean_loss: float32 [], replicated
All inputs are finite; a program needn't handle non-finite values.
Results may differ from a plain program's by a relative error of at most 0.00055.
Values may be sent and summed in bfloat16 or wider, within the bound.
No kernel may reach another device: no remote copies, remote signals or barrier semaphores. Data moves between devices by JAX's collectives and lax.ppermute only.
A program may use at most 64 MiB of HBM per device.

v0:
```python
import jax
import jax.numpy as jnp
from jax import lax
from jax.sharding import PartitionSpec as P


def picked_of(logits, wanted, global_ids):
    matches = wanted[:, None] == global_ids[None, :]
    return jnp.sum(jnp.where(matches, logits, jnp.zeros_like(logits)), axis=1)


def scores(left_rows, right_rows):
    return lax.dot_general(
        left_rows, right_rows, (((1,), (1,)), ((), ())), preferred_element_type=jnp.float32
    )


def local(hidden, embedding, targets):
    vocab_count = lax.axis_size("vocab")
    vocab_index = lax.axis_index("vocab")
    group_index = lax.axis_index("dp")
    tok_dev = hidden.shape[0]
    shard_rows = embedding.shape[0]
    device_index = group_index * vocab_count + vocab_index
    global_ids = device_index * shard_rows + jnp.arange(shard_rows, dtype=jnp.int32)
    logits = scores(lax.all_gather(hidden, ("dp", "vocab"), axis=0, tiled=True), embedding)
    maxima = lax.pmax(jnp.max(logits, axis=1), ("dp", "vocab"))
    local_totals = jnp.sum(jnp.exp(logits - maxima[:, None]), axis=1)
    local_picked = picked_of(logits, targets, global_ids)
    totals, picked = lax.psum((local_totals, local_picked), ("dp", "vocab"))
    losses = maxima + jnp.log(totals) - picked
    mean_loss = jnp.sum(losses) / losses.shape[0]
    token_loss = lax.dynamic_slice_in_dim(losses, device_index * tok_dev, tok_dev)
    return (token_loss, mean_loss)


def solution(mesh):
    return jax.shard_map(
        local,
        mesh=mesh,
        in_specs=(P(("dp", "vocab"), None), P(("dp", "vocab"), None), P()),
        out_specs=(P(("dp", "vocab")), P()),
        check_vma=False,
    )
```

profile of v0, /device:TPU:0, one launch (start us, length us, event | category | flops | bytes accessed | tf_op | source)
XLA Modules:
  0.0 207.5 jit_solution(15314080642424589533)
XLA Ops:
  7.2 0.0 copy-start
  7.2 0.0 all-gather.2.cloned.1.call-start
  7.2 0.7 all-gather.2.cloned.1.call-update
  7.9 0.0 copy-start.1
  7.9 100.9 %all-gather.2.cloned.1.call-done = bf16[1536,4096]{1,0:T(8,128)(2,1)} async-done(((bf16[48,4096]{1,0:T(8,128)(2,1)}), bf16[1536,4096]{1,0:T(8,128)(2,1)}) %all-gather.2.cloned.1.call-update) | async-done | bytes 12582928 | tf_op jit(solution)/shard_map/all_gather | solution.py:26
  108.8 0.0 copy-done
  108.8 7.7 %fusion.1 = (f32[1536]{0:T(1024)S(1)}, f32[1536,256]{0,1:T(8,128)}) fusion(bf16[1536,4096]{1,0:T(8,128)(2,1)} %all-gather.2.cloned.1.call-done, bf16[256,4096]{1,0:T(8,128)(2,1)S(1)} %copy-done), kind=kOutput, calls=%fused_computation.5 | convolution fusion | flops 3221617152 | bytes 16259072 | tf_op jit(solution)/shard_map/dot_general | solution.py:13
  116.5 38.9 %pmax.7 = f32[1536]{0:T(1024)S(1)} all-reduce(f32[1536]{0:T(1024)S(1)} %get-tuple-element.8), channel_id=1, replica_groups=mesh['dp'=2,'vocab'=16] {'dp','vocab'}, use_global_device_ids=true, to_apply=%region_1.0 | all-reduce | flops 1536 | bytes 12288 | tf_op jit(solution)/shard_map/pmax | solution.py:27
  155.5 0.0 copy-done.1
  155.5 1.8 exponential_reduce_fusion
  157.3 40.4 %all-reduce = (f32[1536]{0:T(1024)S(1)}, f32[1536]{0:T(1024)S(1)}) all-reduce(f32[1536]{0:T(1024)S(1)} %get-tuple-element.3, f32[1536]{0:T(1024)S(1)} %get-tuple-element.2), channel_id=1, replica_groups=mesh['dp'=2,'vocab'=16] {'dp','vocab'}, use_global_device_ids=true, to_apply=%region_5.6 | all-reduce | flops 3072 | bytes 24576 | tf_op jit(solution)/shard_map/psum | solution.py:30
  197.7 0.6 fusion
  198.3 0.6 dynamic_slice.3
  (1 shorter events, 0.0 us)
Async XLA Ops:
  7.2 101.7 %copy-start = (bf16[256,4096]{1,0:T(8,128)(2,1)S(1)}, bf16[256,4096]{1,0:T(8,128)(2,1)}, u32[]{:S(2)}) copy-start(bf16[256,4096]{1,0:T(8,128)(2,1)} %param.4) | copy-start | bytes 6291460
  7.2 101.6 %all-gather.2.cloned.1.call-start = ((), (), s32[]{:S(2)}) async-start(), calls=%async_computation | async-start | bytes 12976128 | tf_op jit(solution)/shard_map/all_gather | solution.py:26
  7.9 147.5 %copy-start.1 = (s32[1536]{0:T(1024)S(1)}, s32[1536]{0:T(1024)}, u32[]{:S(2)}) copy-start(s32[1536]{0:T(1024)} %param.5) | copy-start | bytes 18436
Sparse Core Ops, SparseCore 0:
  10.9 97.8 all-gather.1
where the time goes:
time: 208 us; the launch traced here: 207 us
  waiting for transfers between devices  102 us (49%)
  blocking collectives  79.3 us (38%)
  between operations  15.8 us (8%)
  matrix products  7.73 us (4%)
  other arithmetic  2.41 us (1%)
    all_gather x1, waiting for transfers between devices, local(): lax.all_gather(hidden, ('dp', 'vocab'), axis=0, tiled=True)  101 us
    psum x1, blocking collectives, local(): totals, picked = lax.psum((local_totals, local_picked), ('dp', 'vocab'))  40.4 us
    pmax x1, blocking collectives, local(): maxima = lax.pmax(jnp.max(logits, axis=1), ('dp', 'vocab'))  38.9 us
    dot_general x1, matrix products, scores(): lax.dot_general(left_rows, right_rows, (((1,), (1,)), ((), ())), preferre...  7.73 us
  transfers between devices with their start and end apart: 1, of which 1 were waited for; matrix products, arithmetic and copies ran while one was open for 0% of the time, Pallas kernels for 0%

commit v1 on v0

--- a/solution.py
+++ b/solution.py
@@ -2,6 +2,8 @@
 import jax.numpy as jnp
 from jax import lax
 from jax.sharding import PartitionSpec as P
+
+solve_spots = lambda shard_in: lax.psum(lax.psum(shard_in, "vocab"), "dp")
 
 
 def picked_of(logits, wanted, global_ids):
@@ -27,7 +29,7 @@
     maxima = lax.pmax(jnp.max(logits, axis=1), ("dp", "vocab"))
     local_totals = jnp.sum(jnp.exp(logits - maxima[:, None]), axis=1)
     local_picked = picked_of(logits, targets, global_ids)
-    totals, picked = lax.psum((local_totals, local_picked), ("dp", "vocab"))
+    totals, picked = solve_spots((local_totals, local_picked))
     losses = maxima + jnp.log(totals) - picked
     mean_loss = jnp.sum(losses) / losses.shape[0]
     token_loss = lax.dynamic_slice_in_dim(losses, device_index * tok_dev, tok_dev)

time: 208 us -> 234 us (1.12)
  blocking collectives: 79.3 us -> 106 us
    psum x1 -> x2, blocking collectives: 40.4 us -> 67 us  [solve_spots = lambda shard_in: lax.psum(lax.psum(shard_in, 'vocab'), 'dp')]
where the time goes in v1:
time: 234 us
  blocking collectives  106 us (45%)
  waiting for transfers between devices  102 us (44%)
  between operations  15.8 us (7%)
  matrix products  7.73 us (3%)
  other arithmetic  2.41 us (1%)
    all_gather x1, waiting for transfers between devices, local(): lax.all_gather(hidden, ('dp', 'vocab'), axis=0, tiled=True)  101 us
    psum x2, blocking collectives, solve_spots = lambda shard_in: lax.psum(lax.psum(shard_in, 'vocab'), 'dp')  67 us
    pmax x1, blocking collectives, local(): maxima = lax.pmax(jnp.max(logits, axis=1), ('dp', 'vocab'))  38.9 us
    dot_general x1, matrix products, scores(): lax.dot_general(left_rows, right_rows, (((1,), (1,)), ((), ())), preferre...  7.73 us
  transfers between devices with their start and end apart: 1, of which 1 were waited for; matrix products, arithmetic and copies ran while one was open for 0% of the time, Pallas kernels for 0%

profile of v1, /device:TPU:0, one launch (start us, length us, event | category | flops | bytes accessed | tf_op | source)
XLA Modules:
  0.0 234.1 jit_solution(13107249898507563873)
XLA Ops:
  7.2 0.0 copy-start
  7.2 0.0 all-gather.2.cloned.1.call-start
  7.2 0.7 all-gather.2.cloned.1.call-update
  7.9 0.0 copy-start.1
  7.9 100.9 %all-gather.2.cloned.1.call-done = bf16[1536,4096]{1,0:T(8,128)(2,1)} async-done(((bf16[48,4096]{1,0:T(8,128)(2,1)}), bf16[1536,4096]{1,0:T(8,128)(2,1)}) %all-gather.2.cloned.1.call-update) | async-done | bytes 12582928 | tf_op jit(solution)/shard_map/all_gather | solution.py:28
  108.8 0.0 copy-done
  108.8 7.7 %fusion.1 = (f32[1536]{0:T(1024)S(1)}, f32[1536,256]{0,1:T(8,128)}) fusion(bf16[1536,4096]{1,0:T(8,128)(2,1)} %all-gather.2.cloned.1.call-done, bf16[256,4096]{1,0:T(8,128)(2,1)S(1)} %copy-done), kind=kOutput, calls=%fused_computation.5 | convolution fusion | flops 3221617152 | bytes 16259072 | tf_op jit(solution)/shard_map/dot_general | solution.py:15
  116.5 38.9 %pmax.7 = f32[1536]{0:T(1024)S(1)} all-reduce(f32[1536]{0:T(1024)S(1)} %get-tuple-element.10), channel_id=1, replica_groups=mesh['dp'=2,'vocab'=16] {'dp','vocab'}, use_global_device_ids=true, to_apply=%region_1.0 | all-reduce | flops 1536 | bytes 12288 | tf_op jit(solution)/shard_map/pmax | solution.py:29
  155.5 0.0 copy-done.1
  155.5 1.8 exponential_reduce_fusion
  157.3 60.0 %all-reduce = (f32[1536]{0:T(1024)S(1)}, f32[1536]{0:T(1024)S(1)}) all-reduce(f32[1536]{0:T(1024)S(1)} %get-tuple-element.3, f32[1536]{0:T(1024)S(1)} %get-tuple-element.2), channel_id=1, replica_groups=mesh['dp'=2,'vocab'=16] {'vocab'}, use_global_device_ids=true, to_apply=%region_6.7 | all-reduce | flops 3072 | bytes 24576 | tf_op jit(solution)/shard_map/psum | solution.py:6
  217.3 7.0 %all-reduce.1 = (f32[1536]{0:T(1024)S(1)}, f32[1536]{0:T(1024)S(1)}) all-reduce(f32[1536]{0:T(1024)S(1)} %get-tuple-element.4, f32[1536]{0:T(1024)S(1)} %get-tuple-element.5), channel_id=1, replica_groups=mesh['dp'=2,'vocab'=16] {'dp'}, use_global_device_ids=true, to_apply=%region_7.8 | all-reduce | flops 3072 | bytes 24576 | tf_op jit(solution)/shard_map/psum | solution.py:6
  224.3 0.6 fusion
  224.9 0.6 dynamic_slice.3
  (1 shorter events, 0.0 us)
Async XLA Ops:
  7.2 101.7 %copy-start = (bf16[256,4096]{1,0:T(8,128)(2,1)S(1)}, bf16[256,4096]{1,0:T(8,128)(2,1)}, u32[]{:S(2)}) copy-start(bf16[256,4096]{1,0:T(8,128)(2,1)} %param.4) | copy-start | bytes 6291460
  7.2 101.6 %all-gather.2.cloned.1.call-start = ((), (), s32[]{:S(2)}) async-start(), calls=%async_computation | async-start | bytes 12976128 | tf_op jit(solution)/shard_map/all_gather | solution.py:28
  7.9 147.5 %copy-start.1 = (s32[1536]{0:T(1024)S(1)}, s32[1536]{0:T(1024)}, u32[]{:S(2)}) copy-start(s32[1536]{0:T(1024)} %param.5) | copy-start | bytes 18436
Sparse Core Ops, SparseCore 0:
  10.9 97.8 all-gather.1
